TPU v7x, 32 devices: a whole 2x2x4 slice. The times are simulated.
32 devices in a mesh: band: 8 (over z, core), lane: 4 (over y, x).
Axes of the slice: x: 2, y: 2, z: 4, core: 2. Of those that a mesh axis runs over, the one named last changes fastest.
Arguments:
- first_factor: bfloat16 [8192, 4096], P('band', 'lane'), may hold values from -6 to 6
- second_factor: bfloat16 [4096, 2048], P('band', 'lane'), may hold values from -0.09375 to 0.09375
- result_in: float32 [8192, 2048], P('band', 'lane'), may hold values from -6 to 6
- pivot_scale: float32 [4096], replicated, may hold values from 0.25 to 1.75
Outputs:
- updated: float32 [8192, 2048], P('band', 'lane')
All inputs are finite; a program needn't handle non-finite values.
Results may differ from a plain program's by a relative error of at most 0.002.
Values may be sent and summed in bfloat16 or wider, within the bound.
A program may use at most 128 MiB of HBM per device.

v0:
```python
import jax
import jax.numpy as jnp
from jax import lax
from jax.sharding import PartitionSpec as P


def join_panel(left_panel, right_panel):
    return jnp.dot(left_panel, right_panel, preferred_element_type=jnp.float32)


def on_device(first_factor, second_factor, result_in, pivot_scale):
    share = first_factor.shape[1]
    part_scale = lax.dynamic_slice_in_dim(pivot_scale, lax.axis_index("lane") * share, share)
    scaled_left = (first_factor.astype(jnp.float32) * part_scale).astype(jnp.bfloat16)
    left_line = lax.all_gather(scaled_left, "lane", axis=1, tiled=True)
    total = join_panel(left_line, lax.all_gather(second_factor, "band", axis=0, tiled=True))
    updated = result_in - total
    row_power = lax.psum(jnp.sum(updated * updated, axis=1), "lane")
    updated = (
        updated * lax.rsqrt(row_power / (updated.shape[1] * lax.axis_size("lane")) + 1e-06)[:, None]
    )
    return updated


def solution(mesh):
    return jax.shard_map(
        on_device,
        mesh=mesh,
        in_specs=(P("band", "lane"), P("band", "lane"), P("band", "lane"), P()),
        out_specs=P("band", "lane"),
        check_vma=False,
    )
```

profile of v0, /device:TPU:0, one launch (start us, length us, event | category | flops | bytes accessed | tf_op | source)
XLA Modules:
  0.0 177.2 jit_solution(5245780658395474004)
XLA Ops:
  6.5 0.0 all-gather.5.cloned.1.call-start
  6.5 0.7 all-gather.5.cloned.1.call-update
  7.3 0.0 all-gather.3.cloned.1.call-start
  7.3 0.7 dynamic_slice.3
  8.0 3.5 %multiply_convert_fusion = bf16[1024,1024]{1,0:T(8,128)(2,1)} fusion(bf16[1024,1024]{1,0:T(8,128)(2,1)} %param.4, f32[1024]{0:T(1024)S(1)} %dynamic_slice.3), kind=kLoop, calls=%fused_computation | loop fusion | flops 3145728 | bytes 4198400 | tf_op jit(solution)/shard_map/convert_element_type | solution.py:14
  11.5 0.0 copy-start
  11.5 0.0 all-gather.3.cloned.1.call-update
  11.5 1.6 copy-done
  13.1 1.8 %copy.5 = f32[1024,512]{0,1:T(8,128)} copy(f32[1024,512]{1,0:T(8,128)S(1)} %copy-done) | data formatting | bytes 4194304 | tf_op args[2]
  14.9 43.7 %all-gather.5.cloned.1.call-done = bf16[4096,512]{1,0:T(8,128)(2,1)} async-done(((bf16[512,512]{1,0:T(8,128)(2,1)}), bf16[4096,512]{1,0:T(8,128)(2,1)}) %all-gather.5.cloned.1.call-update) | async-done | bytes 4194320 | tf_op jit(solution)/shard_map/all_gather | solution.py:16
  58.6 88.2 %all-gather.3.cloned.1.call-done = bf16[1024,4096]{1,0:T(8,128)(2,1)} async-done(((bf16[1024,1024]{1,0:T(8,128)(2,1)}), bf16[1024,4096]{1,0:T(8,128)(2,1)}) %all-gather.3.cloned.1.call-update) | async-done | bytes 8388624 | tf_op jit(solution)/shard_map/all_gather | solution.py:15
  146.7 11.1 %multiply_reduce_fusion = (f32[1024]{0:T(1024)S(1)}, f32[1024,512]{0,1:T(8,128)}) fusion(f32[1024,512]{0,1:T(8,128)} %copy.5, bf16[1024,4096]{1,0:T(8,128)(2,1)} %all-gather.3.cloned.1.call-done, bf16[4096,512]{1,0:T(8,128)(2,1)} %all-gather.5.cloned.1.call-done), kind=kOutput, calls=%fused_computation.1 | convolution fusion | flops 4296539136 | bytes 16781312 | tf_op jit(solution)/shard_map/dot_general | solution.py:8
  157.8 8.9 %psum.7 = f32[1024]{0:T(1024)S(1)} all-reduce(f32[1024]{0:T(1024)S(1)} %get-tuple-element.5), channel_id=1, replica_groups=mesh['band'=8,'lane'=4] {'lane'}, use_global_device_ids=true, to_apply=%region_1.0 | all-reduce | flops 1024 | bytes 8192 | tf_op jit(solution)/shard_map/psum | solution.py:18
  166.7 1.8 %broadcast_multiply_fusion = f32[1024,512]{0,1:T(8,128)S(1)} fusion(f32[1024,512]{0,1:T(8,128)} %get-tuple-element.6, f32[1024]{0:T(1024)S(1)} %add_rsqrt_fusion), kind=kLoop, calls=%fused_computation.3 | loop fusion | flops 524288 | bytes 4198400 | tf_op jit(solution)/shard_map/mul | solution.py:20
  168.6 1.8 %copy.6 = f32[1024,512]{1,0:T(8,128)} copy(f32[1024,512]{0,1:T(8,128)S(1)} %broadcast_multiply_fusion) | data formatting | bytes 4194304 | tf_op jit(solution)/shard_map/mul | solution.py:20
  (1 shorter events, 0.0 us)
Async XLA Ops:
  6.5 52.0 %all-gather.5.cloned.1.call-start = ((), (), s32[]{:S(2)}) async-start(), calls=%async_computation.1 | async-start | bytes 4718592 | tf_op jit(solution)/shard_map/all_gather | solution.py:16
  7.3 139.5 %all-gather.3.cloned.1.call-start = ((), (), s32[]{:S(2)}) async-start(), calls=%async_computation | async-start | bytes 10485760 | tf_op jit(solution)/shard_map/all_gather | solution.py:15
  11.5 1.6 copy-start
Sparse Core Ops, SparseCore 0:
  8.9 49.5 all-gather.4
  60.4 86.2 all-gather.2
where the time goes:
time: 177 us
  waiting for transfers between devices  133 us (75%)
  between operations  13.4 us (8%)
  matrix products  11.1 us (6%)
  blocking collectives  8.9 us (5%)
  local copies, waits for them, and re-layouts  5.88 us (3%)
  other arithmetic  5.32 us (3%)
    all_gather x1, waiting for transfers between devices, on_device(): left_line = lax.all_gather(scaled_left, 'lane', axis=1, tiled=True)  88.2 us
    all_gather x1, waiting for transfers between devices, on_device(): lax.all_gather(second_factor, 'band', axis=0, tiled=True)  43.7 us
    dot_general x1, matrix products, join_panel(): return jnp.dot(left_panel, right_panel, preferred_element_type=jnp.float32)  11.1 us
    psum x1, blocking collectives, on_device(): row_power = lax.psum(jnp.sum(updated * updated, axis=1), 'lane')  8.9 us
  transfers between devices with their start and end apart: 2, of which 2 were waited for; matrix products, arithmetic and copies ran while one was open for 3% of the time, Pallas kernels for 0%

commit v1 on v0

--- a/solution.py
+++ b/solution.py
@@ -13,7 +13,20 @@
     part_scale = lax.dynamic_slice_in_dim(pivot_scale, lax.axis_index("lane") * share, share)
     scaled_left = (first_factor.astype(jnp.float32) * part_scale).astype(jnp.bfloat16)
     left_line = lax.all_gather(scaled_left, "lane", axis=1, tiled=True)
-    total = join_panel(left_line, lax.all_gather(second_factor, "band", axis=0, tiled=True))
+
+    def choose_shards(a_name, inp):
+        f_now, t_next, out_arr = (lax.axis_size(a_name), lax.axis_index(a_name), inp.shape[0])
+        pieces_in = tuple(((ii, (ii + 1) % f_now) for ii in range(f_now)))
+        z2 = jnp.zeros((*inp.shape[:0], f_now * out_arr, *inp.shape[1:]), inp.dtype)
+        a_now = inp
+        for s in range(f_now):
+            w2 = (t_next - s) % f_now
+            z2 = lax.dynamic_update_slice_in_dim(z2, a_now, w2 * out_arr, axis=0)
+            if s < f_now - 1:
+                a_now = lax.ppermute(a_now, a_name, pieces_in)
+        return z2
+
+    total = join_panel(left_line, choose_shards("band", second_factor))
     updated = result_in - total
     row_power = lax.psum(jnp.sum(updated * updated, axis=1), "lane")
     updated = (

time: 177 us -> 131 us (0.74)
  waiting for transfers between devices: 133 us -> 74.5 us
  local copies, waits for them, and re-layouts: 5.88 us -> 17.9 us
    all_gather x1, waiting for transfers between devices: 88.2 us -> 13.3 us  [on_device(): left_line = lax.all_gather(scaled_left, 'lane', axis=1, tiled=True)]
    ppermute x0 -> x7, waiting for transfers between devices: none -> 61.2 us  [choose_shards(): a_now = lax.ppermute(a_now, a_name, pieces_in)]
    all_gather x1 -> x0, waiting for transfers between devices: 43.7 us -> none  [on_device(): lax.all_gather(second_factor, 'band', axis=0, tiled=True)]
    dynamic_update_slice x0 -> x8, local copies, waits for them, and re-layouts: none -> 8.78 us  [choose_shards(): z2 = lax.dynamic_update_slice_in_dim(z2, a_now, w2 * out_arr, axis=0)]
    broadcast_in_dim x0 -> x1, local copies, waits for them, and re-layouts: none -> 2.24 us  [choose_shards(): z2 = jnp.zeros((*inp.shape[:0], f_now * out_arr, *inp.shape[1:]), inp.dtype)]
    unnamed x3 -> x19, local copies, waits for them, and re-layouts: 3.37 us -> 4.25 us
  transfers between devices with their start and end apart: 2 -> 8, of which waited for: 2 -> 8; matrix products, arithmetic and copies ran while one was open for 3% -> 10% of each run, Pallas kernels for 0% -> 0%
where the time goes in v1:
time: 131 us
  waiting for transfers between devices  74.5 us (57%)
  local copies, waits for them, and re-layouts  17.9 us (14%)
  between operations  13.4 us (10%)
  matrix products  10.4 us (8%)
  blocking collectives  8.9 us (7%)
  other arithmetic  5.41 us (4%)
    ppermute x7, waiting for transfers between devices, choose_shards(): a_now = lax.ppermute(a_now, a_name, pieces_in)  61.2 us
    all_gather x1, waiting for transfers between devices, on_device(): left_line = lax.all_gather(scaled_left, 'lane', axis=1, tiled=True)  13.3 us
    dot_general x1, matrix products, join_panel(): return jnp.dot(left_panel, right_panel, preferred_element_type=jnp.float32)  10.4 us
    psum x1, blocking collectives, on_device(): row_power = lax.psum(jnp.sum(updated * updated, axis=1), 'lane')  8.9 us
    dynamic_update_slice x8, local copies, waits for them, and re-layouts, choose_shards(): z2 = lax.dynamic_update_slice_in_dim(z2, a_now, w2 * out_arr, axis=0)  8.78 us
    unnamed x19, local copies, waits for them, and re-layouts  4.25 us
    convert_element_type x1, other arithmetic, on_device(): (first_factor.astype(jnp.float32) * part_scale).astype(jnp.bfloat16)  3.48 us
  transfers between devices with their start and end apart: 8, of which 8 were waited for; matrix products, arithmetic and copies ran while one was open for 10% of the time, Pallas kernels for 0%

profile of v1, /device:TPU:0, one launch (start us, length us, event | category | flops | bytes accessed | tf_op | source)
XLA Modules:
  0.0 131.2 jit_solution(17002306668225690973)
XLA Ops:
  6.5 0.8 dynamic_slice.3
  7.4 3.5 %multiply_convert_fusion = bf16[1024,1024]{1,0:T(8,128)(2,1)} fusion(bf16[1024,1024]{1,0:T(8,128)(2,1)} %param.4, f32[1024]{0:T(1024)S(1)} %dynamic_slice.3), kind=kLoop, calls=%fused_computation | loop fusion | flops 3145728 | bytes 4198400 | tf_op jit(solution)/shard_map/convert_element_type | solution.py:14
  11.4 10.9 %collective-permute-done = bf16[512,512]{1,0:T(8,128)(2,1)S(1)} collective-permute-done((bf16[512,512]{1,0:T(8,128)(2,1)S(1)}, bf16[512,512]{1,0:T(8,128)(2,1)S(1)}, u32[]{:S(2)}, u32[]{:S(2)}) %collective-permute-start) | collective-permute-done | bytes 524320 | tf_op jit(solution)/shard_map/ppermute | solution.py:26
  23.1 9.6 %collective-permute-done.1 = bf16[512,512]{1,0:T(8,128)(2,1)S(1)} collective-permute-done((bf16[512,512]{1,0:T(8,128)(2,1)S(1)}, bf16[512,512]{1,0:T(8,128)(2,1)S(1)}, u32[]{:S(2)}, u32[]{:S(2)}) %collective-permute-start.1) | collective-permute-done | bytes 524320 | tf_op jit(solution)/shard_map/ppermute | solution.py:26
  32.7 10.4 %collective-permute-done.2 = bf16[512,512]{1,0:T(8,128)(2,1)S(1)} collective-permute-done((bf16[512,512]{1,0:T(8,128)(2,1)S(1)}, bf16[512,512]{1,0:T(8,128)(2,1)S(1)}, u32[]{:S(2)}, u32[]{:S(2)}) %collective-permute-start.2) | collective-permute-done | bytes 524320 | tf_op jit(solution)/shard_map/ppermute | solution.py:26
  44.0 10.4 %collective-permute-done.3 = bf16[512,512]{1,0:T(8,128)(2,1)S(1)} collective-permute-done((bf16[512,512]{1,0:T(8,128)(2,1)S(1)}, bf16[512,512]{1,0:T(8,128)(2,1)S(1)}, u32[]{:S(2)}, u32[]{:S(2)}) %collective-permute-start.3) | collective-permute-done | bytes 524320 | tf_op jit(solution)/shard_map/ppermute | solution.py:26
  54.4 0.8 copy-done.7
  55.2 10.5 %collective-permute-done.4 = bf16[512,512]{1,0:T(8,128)(2,1)} collective-permute-done((bf16[512,512]{1,0:T(8,128)(2,1)S(1)}, bf16[512,512]{1,0:T(8,128)(2,1)}, u32[]{:S(2)}, u32[]{:S(2)}) %collective-permute-start.4) | collective-permute-done | bytes 524320 | tf_op jit(solution)/shard_map/ppermute | solution.py:26
  65.7 1.8 %copy.5 = f32[1024,512]{0,1:T(8,128)} copy(f32[1024,512]{1,0:T(8,128)S(1)} %copy-done) | data formatting | bytes 4194304 | tf_op args[2]
  67.5 2.2 %broadcast_in_dim.2 = bf16[4096,512]{1,0:T(8,128)(2,1)} broadcast(bf16[]{:T(256)} %constant.71.clone.1), dimensions={} | broadcast | bytes 4194306 | tf_op jit(solution)/shard_map/broadcast_in_dim | solution.py:20
  69.8 0.9 constant_dynamic-update-slice_fusion.7
  70.6 0.8 constant_dynamic-update-slice_fusion.6
  71.4 5.0 %collective-permute-done.5 = bf16[512,512]{1,0:T(8,128)(2,1)} collective-permute-done((bf16[512,512]{1,0:T(8,128)(2,1)}, bf16[512,512]{1,0:T(8,128)(2,1)}, u32[]{:S(2)}, u32[]{:S(2)}) %collective-permute-start.5) | collective-permute-done | bytes 524320 | tf_op jit(solution)/shard_map/ppermute | solution.py:26
  76.4 0.8 constant_dynamic-update-slice_fusion.5
  78.1 0.8 constant_dynamic-update-slice_fusion.3
  78.9 1.9 %constant_dynamic-update-slice_fusion.2 = bf16[4096,512]{1,0:T(8,128)(2,1)} fusion(bf16[4096,512]{1,0:T(8,128)(2,1)} %constant_dynamic-update-slice_fusion.3, bf16[512,512]{1,0:T(8,128)(2,1)} %collective-permute-done.4, s32[]{:T(128)S(6)} %select_n.74), kind=kLoop, calls=%fused_computation.7 | loop fusion | bytes 1048580 | tf_op jit(solution)/shard_map/dynamic_update_slice | solution.py:24
  80.8 1.9 %constant_dynamic-update-slice_fusion.1 = bf16[4096,512]{1,0:T(8,128)(2,1)} fusion(bf16[4096,512]{1,0:T(8,128)(2,1)} %constant_dynamic-update-slice_fusion.2, bf16[512,512]{1,0:T(8,128)(2,1)} %collective-permute-done.5, s32[]{:T(128)S(6)} %select_n.76), kind=kLoop, calls=%fused_computation.6 | loop fusion | bytes 1048580 | tf_op jit(solution)/shard_map/dynamic_update_slice | solution.py:24
  82.7 4.4 %collective-permute-done.6 = bf16[512,512]{1,0:T(8,128)(2,1)S(1)} collective-permute-done((bf16[512,512]{1,0:T(8,128)(2,1)}, bf16[512,512]{1,0:T(8,128)(2,1)S(1)}, u32[]{:S(2)}, u32[]{:S(2)}) %collective-permute-start.6) | collective-permute-done | bytes 524320 | tf_op jit(solution)/shard_map/ppermute | solution.py:26
  87.0 0.9 constant_dynamic-update-slice_fusion
  87.9 13.3 %all-gather.2.cloned.1.call-done = bf16[1024,4096]{1,0:T(8,128)(2,1)} async-done(((bf16[1024,1024]{1,0:T(8,128)(2,1)}), bf16[1024,4096]{1,0:T(8,128)(2,1)}) %all-gather.2.cloned.1.call-update) | async-done | bytes 8388624 | tf_op jit(solution)/shard_map/all_gather | solution.py:15
  101.2 10.4 %multiply_reduce_fusion = (f32[1024]{0:T(1024)S(1)}, f32[1024,512]{0,1:T(8,128)}) fusion(f32[1024,512]{0,1:T(8,128)S(1)} %copy-done.1, bf16[1024,4096]{1,0:T(8,128)(2,1)} %all-gather.2.cloned.1.call-done, bf16[4096,512]{1,0:T(8,128)(2,1)} %constant_dynamic-update-slice_fusion), kind=kOutput, calls=%fused_computation.1 | convolution fusion | flops 4296539136 | bytes 16781312 | tf_op jit(solution)/shard_map/dot_general | solution.py:8
  111.7 8.9 %psum.7 = f32[1024]{0:T(1024)S(1)} all-reduce(f32[1024]{0:T(1024)S(1)} %get-tuple-element.5), channel_id=1, replica_groups=mesh['band'=8,'lane'=4] {'lane'}, use_global_device_ids=true, to_apply=%region_1.2 | all-reduce | flops 1024 | bytes 8192 | tf_op jit(solution)/shard_map/psum | solution.py:31
  120.6 1.9 %broadcast_multiply_fusion = f32[1024,512]{0,1:T(8,128)S(1)} fusion(f32[1024,512]{0,1:T(8,128)} %get-tuple-element.6, f32[1024]{0:T(1024)S(1)} %add_rsqrt_fusion), kind=kLoop, calls=%fused_computation.3 | loop fusion | flops 524288 | bytes 4198400 | tf_op jit(solution)/shard_map/mul | solution.py:33
  122.5 1.8 %copy.6 = f32[1024,512]{1,0:T(8,128)} copy(f32[1024,512]{0,1:T(8,128)S(1)} %broadcast_multiply_fusion) | data formatting | bytes 4194304 | tf_op jit(solution)/shard_map/mul | solution.py:33
  (28 shorter events, 3.0 us)
Async XLA Ops:
  6.5 4.4 %copy-start.2 = (bf16[512,512]{1,0:T(8,128)(2,1)S(1)}, bf16[512,512]{1,0:T(8,128)(2,1)}, u32[]{:S(2)}) copy-start(bf16[512,512]{1,0:T(8,128)(2,1)} %param.5) | copy-start | bytes 1572868
  6.5 59.2 %copy-start = (f32[1024,512]{1,0:T(8,128)S(1)}, f32[1024,512]{1,0:T(8,128)}, u32[]{:S(2)}) copy-start(f32[1024,512]{1,0:T(8,128)} %param.6) | copy-start | bytes 6291460
  6.5 94.7 %all-gather.2.cloned.1.call-start = ((), (), s32[]{:S(2)}) async-start(), calls=%async_computation | async-start | bytes 10485760 | tf_op jit(solution)/shard_map/all_gather | solution.py:15
  10.9 11.4 %collective-permute-start = (bf16[512,512]{1,0:T(8,128)(2,1)S(1)}, bf16[512,512]{1,0:T(8,128)(2,1)S(1)}, u32[]{:S(2)}, u32[]{:S(2)}) collective-permute-start(bf16[512,512]{1,0:T(8,128)(2,1)S(1)} %copy-done.2), channel_id=1, source_target_pairs={{0,4},{4,8},{8,12},{12,16},{16,20},{20,24},{24,28},{28,0},{1,5},{5... | collective-permute-start | bytes 1572872 | tf_op jit(solution)/shard_map/ppermute | solution.py:26
  22.3 0.8 copy-start.5
  22.3 10.4 %collective-permute-start.1 = (bf16[512,512]{1,0:T(8,128)(2,1)S(1)}, bf16[512,512]{1,0:T(8,128)(2,1)S(1)}, u32[]{:S(2)}, u32[]{:S(2)}) collective-permute-start(bf16[512,512]{1,0:T(8,128)(2,1)S(1)} %collective-permute-done), channel_id=1, source_target_pairs={{0,4},{4,8},{8,12},{12,16},{16,20},{20,24},{24,28},{28,0},{1,5},{5... | collective-permute-start | bytes 1572872 | tf_op jit(solution)/shard_map/ppermute | solution.py:26
  32.7 10.4 %collective-permute-start.2 = (bf16[512,512]{1,0:T(8,128)(2,1)S(1)}, bf16[512,512]{1,0:T(8,128)(2,1)S(1)}, u32[]{:S(2)}, u32[]{:S(2)}) collective-permute-start(bf16[512,512]{1,0:T(8,128)(2,1)S(1)} %collective-permute-done.1), channel_id=1, source_target_pairs={{0,4},{4,8},{8,12},{12,16},{16,20},{20,24},{24,28},{28,0},{1,5},{5... | collective-permute-start | bytes 1572872 | tf_op jit(solution)/shard_map/ppermute | solution.py:26
  43.1 0.8 copy-start.3
  44.0 10.4 %collective-permute-start.3 = (bf16[512,512]{1,0:T(8,128)(2,1)S(1)}, bf16[512,512]{1,0:T(8,128)(2,1)S(1)}, u32[]{:S(2)}, u32[]{:S(2)}) collective-permute-start(bf16[512,512]{1,0:T(8,128)(2,1)S(1)} %collective-permute-done.2), channel_id=1, source_target_pairs={{0,4},{4,8},{8,12},{12,16},{16,20},{20,24},{24,28},{28,0},{1,5},{5... | collective-permute-start | bytes 1572872 | tf_op jit(solution)/shard_map/ppermute | solution.py:26
  54.4 0.8 copy-start.7
  55.2 10.5 %collective-permute-start.4 = (bf16[512,512]{1,0:T(8,128)(2,1)S(1)}, bf16[512,512]{1,0:T(8,128)(2,1)}, u32[]{:S(2)}, u32[]{:S(2)}) collective-permute-start(bf16[512,512]{1,0:T(8,128)(2,1)S(1)} %collective-permute-done.3), channel_id=1, source_target_pairs={{0,4},{4,8},{8,12},{12,16},{16,20},{20,24},{24,28},{28,0},{1,5},{5... | collective-permute-start | bytes 1572872 | tf_op jit(solution)/shard_map/ppermute | solution.py:26
  65.7 10.7 %collective-permute-start.5 = (bf16[512,512]{1,0:T(8,128)(2,1)}, bf16[512,512]{1,0:T(8,128)(2,1)}, u32[]{:S(2)}, u32[]{:S(2)}) collective-permute-start(bf16[512,512]{1,0:T(8,128)(2,1)} %collective-permute-done.4), channel_id=1, source_target_pairs={{0,4},{4,8},{8,12},{12,16},{16,20},{20,24},{24,28},{28,0},{1,5},{5... | collective-permute-start | bytes 1572872 | tf_op jit(solution)/shard_map/ppermute | solution.py:26
  67.5 3.1 %copy-start.6 = (bf16[512,512]{1,0:T(8,128)(2,1)S(1)}, bf16[512,512]{1,0:T(8,128)(2,1)}, u32[]{:S(2)}) copy-start(bf16[512,512]{1,0:T(8,128)(2,1)} %copy-done.5) | copy-start | bytes 1572868
  67.5 9.7 %copy-start.4 = (bf16[512,512]{1,0:T(8,128)(2,1)S(1)}, bf16[512,512]{1,0:T(8,128)(2,1)}, u32[]{:S(2)}) copy-start(bf16[512,512]{1,0:T(8,128)(2,1)} %copy-done.3) | copy-start | bytes 1572868
  67.5 10.6 %copy-start.8 = (bf16[512,512]{1,0:T(8,128)(2,1)S(1)}, bf16[512,512]{1,0:T(8,128)(2,1)}, u32[]{:S(2)}) copy-start(bf16[512,512]{1,0:T(8,128)(2,1)} %copy-done.7) | copy-start | bytes 1572868
  69.8 31.5 %copy-start.1 = (f32[1024,512]{0,1:T(8,128)S(1)}, f32[1024,512]{0,1:T(8,128)}, u32[]{:S(2)}) copy-start(f32[1024,512]{0,1:T(8,128)} %copy.5) | copy-start | bytes 6291460
  76.4 10.6 %collective-permute-start.6 = (bf16[512,512]{1,0:T(8,128)(2,1)}, bf16[512,512]{1,0:T(8,128)(2,1)S(1)}, u32[]{:S(2)}, u32[]{:S(2)}) collective-permute-start(bf16[512,512]{1,0:T(8,128)(2,1)} %collective-permute-done.5), channel_id=1, source_target_pairs={{0,4},{4,8},{8,12},{12,16},{16,20},{20,24},{24,28},{28,0},{1,5},{5... | collective-permute-start | bytes 1572872 | tf_op jit(solution)/shard_map/ppermute | solution.py:26
Sparse Core Ops, SparseCore 0:
  11.0 90.1 all-gather.1
